TPU v7x, 32 devices: a whole 2x2x4 slice. The times are simulated.
32 devices in a mesh: shard: 16 (over z, y, core), model: 2 (over x).
Axes of the slice: x: 2, y: 2, z: 4, core: 2. Of those that a mesh axis runs over, the one named last changes fastest.
Arguments:
- gradients: float32 [128, 128, 4096], P(None, 'shard', 'model'), may hold values from -6 to 6
- momentum: float32 [128, 128, 4096], P(None, 'shard', 'model'), may hold values from -6 to 6
- weights: float32 [128, 128, 4096], P(None, 'shard', 'model'), may hold values from -0.1875 to 0.1875
Outputs:
- new_weights: float32 [128, 128, 4096], P(None, 'shard', 'model')
- new_momentum: float32 [128, 128, 4096], P(None, 'shard', 'model')
All inputs are finite; a program needn't handle non-finite values.
Results may differ from a plain program's by a relative error of at most 0.00012.
Values sent between devices are 32-bit elements; how exact they have to be, the bound alone decides.
A program may use at most 128 MiB of HBM per device.

v0:
```python
import jax
import jax.numpy as jnp
from jax import lax
from jax.sharding import PartitionSpec as P

ITERS = 4


hold_rate = 0.9
learn_rate = 0.8


def local(gradients, momentum, weights):
    new_momentum = hold_rate * momentum + gradients
    direction = hold_rate * new_momentum + gradients
    moved = lax.all_to_all(direction, "shard", split_axis=0, concat_axis=1, tiled=True)
    total = lax.psum(jnp.sum(moved * moved, axis=(1, 2), keepdims=True), "model")
    iterate = moved * lax.rsqrt(total + 1e-06)
    for step in range(ITERS):
        gram = lax.psum(
            jnp.einsum("mik,mjk->mij", iterate, iterate, precision=lax.Precision.HIGHEST), "model"
        )
        mixed = -4.775 * gram + 2.0315 * jnp.einsum(
            "mij,mjk->mik", gram, gram, precision=lax.Precision.HIGHEST
        )
        iterate = 3.4445 * iterate + jnp.einsum(
            "mij,mjk->mik", mixed, iterate, precision=lax.Precision.HIGHEST
        )
    back = lax.all_to_all(iterate, "shard", split_axis=1, concat_axis=0, tiled=True)
    new_weights = weights - learn_rate * back
    return (new_weights, new_momentum)


def solution(mesh):
    return jax.shard_map(
        local,
        mesh=mesh,
        in_specs=(P(None, "shard", "model"), P(None, "shard", "model"), P(None, "shard", "model")),
        out_specs=(P(None, "shard", "model"), P(None, "shard", "model")),
        check_vma=False,
    )
```

profile of v0, /device:TPU:0, one launch (start us, length us, event | category | flops | bytes accessed | tf_op | source)
XLA Modules:
  0.0 666.1 jit_solution(225198048523611833)
XLA Ops:
  7.2 9.3 %multiply_add_fusion.4 = (f32[128,8,2048]{2,1,0:T(8,128)S(1)}, f32[128,8,2048]{2,1,0:T(8,128)}) fusion(f32[128,8,2048]{2,1,0:T(8,128)} %param.3, f32[128,8,2048]{2,1,0:T(8,128)} %param.4), kind=kLoop, calls=%fused_computation.8 | loop fusion | flops 8388608 | bytes 33554432 | tf_op jit(solution)/shard_map/add | solution.py:15
  16.5 189.2 %all_to_all.27 = f32[128,8,2048]{2,1,0:T(8,128)S(1)} all-to-all(f32[128,8,2048]{2,1,0:T(8,128)S(1)} %get-tuple-element.2), channel_id=1, replica_groups=mesh['shard'=16,'model'=2] {'shard'}, dimensions={0} | all-to-all | bytes 16777216 | tf_op jit(solution)/shard_map/all_to_all | solution.py:16
  205.7 3.4 copy-done
  209.9 4.9 psum.35
  214.8 12.9 %fusion.2 = f32[8,128,128]{2,1,0:T(8,128)} fusion(f32[16,8,8,2048]{3,2,1,0:T(8,128)} %bitcast.44, f32[8]{0:T(128)S(1)} %rsqrt_bitcast_fusion), kind=kOutput, calls=%fused_computation.11 | convolution fusion | flops 3223322624 | bytes 8912928 | tf_op jit(solution)/shard_map/mik,mjk->mij/dot_general | solution.py:21
  227.8 29.7 %all-reduce.5.cloned.1.call-done = f32[8,128,128]{2,1,0:T(8,128)} async-done(((f32[8,128,128]{2,1,0:T(8,128)}), f32[8,128,128]{2,1,0:T(8,128)}) %all-reduce.5.cloned.1.call-update) | async-done | bytes 524304 | tf_op jit(solution)/shard_map/psum | solution.py:20
  257.5 2.1 fusion.8
  259.6 11.7 %multiply_add_fusion.3 = f32[8,128,2048]{2,1,0:T(8,128)S(1)} fusion(f32[16,8,8,2048]{3,2,1,0:T(8,128)} %bitcast.45, f32[8,128,128]{2,1,0:T(8,128)S(1)} %fusion.8, f32[8]{0:T(128)S(1)} %rsqrt_bitcast_fusion), kind=kOutput, calls=%fused_computation.7 | convolution fusion | flops 3229614080 | bytes 17301536 | tf_op jit(solution)/shard_map/mij,mjk->mik/dot_general | solution.py:26
  271.3 3.4 copy-done.1
  274.7 8.5 %fusion.9 = f32[8,128,128]{2,1,0:T(8,128)} fusion(f32[8,128,2048]{2,1,0:T(8,128)S(1)} %multiply_add_fusion.3), kind=kOutput, calls=%fused_computation.24 | convolution fusion | flops 3221225472 | bytes 8912896 | tf_op jit(solution)/shard_map/mik,mjk->mij/dot_general | solution.py:21
  283.3 28.8 %all-reduce.7.cloned.1.call-done = f32[8,128,128]{2,1,0:T(8,128)} async-done(((f32[8,128,128]{2,1,0:T(8,128)}), f32[8,128,128]{2,1,0:T(8,128)}) %all-reduce.7.cloned.1.call-update) | async-done | bytes 524304 | tf_op jit(solution)/shard_map/psum | solution.py:20
  314.2 14.3 %multiply_add_fusion.2 = f32[8,128,2048]{2,1,0:T(8,128)S(1)} fusion(f32[8,128,2048]{2,1,0:T(8,128)} %copy-done.1, f32[8,128,128]{2,1,0:T(8,128)S(1)} %fusion.7), kind=kOutput, calls=%fused_computation.6 | convolution fusion | flops 3225419776 | bytes 17301504 | tf_op jit(solution)/shard_map/mij,mjk->mik/dot_general | solution.py:26
  328.5 3.4 copy-done.2
  331.9 8.5 %fusion.10 = f32[8,128,128]{2,1,0:T(8,128)} fusion(f32[8,128,2048]{2,1,0:T(8,128)S(1)} %multiply_add_fusion.2), kind=kOutput, calls=%fused_computation.25 | convolution fusion | flops 3221225472 | bytes 8912896 | tf_op jit(solution)/shard_map/mik,mjk->mij/dot_general | solution.py:21
  340.5 28.8 %all-reduce.9.cloned.1.call-done = f32[8,128,128]{2,1,0:T(8,128)} async-done(((f32[8,128,128]{2,1,0:T(8,128)}), f32[8,128,128]{2,1,0:T(8,128)}) %all-reduce.9.cloned.1.call-update) | async-done | bytes 524304 | tf_op jit(solution)/shard_map/psum | solution.py:20
  371.4 14.1 %multiply_add_fusion.1 = f32[8,128,2048]{2,1,0:T(8,128)S(1)} fusion(f32[8,128,2048]{2,1,0:T(8,128)} %copy-done.2, f32[8,128,128]{2,1,0:T(8,128)S(1)} %fusion.6), kind=kOutput, calls=%fused_computation.5 | convolution fusion | flops 3225419776 | bytes 17301504 | tf_op jit(solution)/shard_map/mij,mjk->mik/dot_general | solution.py:26
  385.5 3.4 copy-done.3
  388.9 8.5 %fusion.11 = f32[8,128,128]{2,1,0:T(8,128)} fusion(f32[8,128,2048]{2,1,0:T(8,128)S(1)} %multiply_add_fusion.1), kind=kOutput, calls=%fused_computation.26 | convolution fusion | flops 3221225472 | bytes 8912896 | tf_op jit(solution)/shard_map/mik,mjk->mij/dot_general | solution.py:21
  397.4 28.8 %all-reduce.11.cloned.1.call-done = f32[8,128,128]{2,1,0:T(8,128)} async-done(((f32[8,128,128]{2,1,0:T(8,128)}), f32[8,128,128]{2,1,0:T(8,128)}) %all-reduce.11.cloned.1.call-update) | async-done | bytes 524304 | tf_op jit(solution)/shard_map/psum | solution.py:20
  428.3 14.9 %multiply_add_fusion = f32[8,128,2048]{2,1,0:T(8,128)S(1)} fusion(f32[8,128,2048]{2,1,0:T(8,128)} %copy-done.3, f32[8,128,128]{2,1,0:T(8,128)S(1)} %fusion.5), kind=kOutput, calls=%fused_computation.4 | convolution fusion | flops 3225419776 | bytes 17301504 | tf_op jit(solution)/shard_map/mij,mjk->mik/dot_general | solution.py:26
  443.2 4.9 copy.8
  448.0 187.7 %all_to_all.28 = f32[8,128,2048]{2,0,1:T(8,128)S(1)} all-to-all(f32[8,128,2048]{2,0,1:T(8,128)S(1)} %copy.8), channel_id=1, replica_groups=mesh['shard'=16,'model'=2] {'shard'}, dimensions={1} | all-to-all | bytes 16777216 | tf_op jit(solution)/shard_map/all_to_all | solution.py:29
  637.5 9.7 %copy.9 = f32[16,8,8,2048]{3,2,1,0:T(8,128)} copy(f32[16,8,8,2048]{3,1,2,0:T(8,128)S(1)} %bitcast.46) | data formatting | bytes 16777216 | tf_op jit(solution)/shard_map/mul | solution.py:30
  647.2 11.9 %bitcast_subtract_fusion = f32[128,8,2048]{2,1,0:T(8,128)} fusion(f32[128,8,2048]{2,1,0:T(8,128)} %param.5, f32[16,8,8,2048]{3,2,1,0:T(8,128)} %copy.9), kind=kLoop, calls=%fused_computation.1 | loop fusion | flops 2097152 | bytes 25165824 | tf_op jit(solution)/shard_map/sub | solution.py:30
  (18 shorter events, 9.1 us)
Async XLA Ops:
  7.2 250.4 %all-reduce.5.cloned.1.call-start = ((), (), s32[]{:S(2)}) async-start(), calls=%async_computation.2 | async-start | bytes 1048576 | tf_op jit(solution)/shard_map/psum | solution.py:20
  205.7 3.4 copy-start
  227.7 84.4 %all-reduce.7.cloned.1.call-start = ((), (), s32[]{:S(2)}) async-start(), calls=%async_computation.3 | async-start | bytes 1048576 | tf_op jit(solution)/shard_map/psum | solution.py:20
  271.3 3.4 copy-start.1
  283.3 86.0 %all-reduce.9.cloned.1.call-start = ((), (), s32[]{:S(2)}) async-start(), calls=%async_computation.4 | async-start | bytes 1048576 | tf_op jit(solution)/shard_map/psum | solution.py:20
  328.5 3.4 copy-start.2
  340.5 85.8 %all-reduce.11.cloned.1.call-start = ((), (), s32[]{:S(2)}) async-start(), calls=%async_computation.5 | async-start | bytes 1048576 | tf_op jit(solution)/shard_map/psum | solution.py:20
  385.5 3.4 copy-start.3
Sparse Core Ops, SparseCore 0:
  227.8 29.6 all-reduce.4
  283.4 28.6 all-reduce.6
  340.6 28.6 all-reduce.8
  397.5 28.6 all-reduce.10
where the time goes:
time: 675 us; the launch traced here: 666 us
  blocking collectives  382 us (57%)
  waiting for transfers between devices  116 us (17%)
  matrix products  102 us (15%)
  local copies, waits for them, and re-layouts  28.1 us (4%)
  other arithmetic  23.8 us (4%)
  between operations  14.3 us (2%)
    all_to_all x1, blocking collectives, local(): lax.all_to_all(direction, 'shard', split_axis=0, concat_axis=1, tiled=True)  189 us
    all_to_all x1, blocking collectives, local(): lax.all_to_all(iterate, 'shard', split_axis=1, concat_axis=0, tiled=True)  188 us
    psum x4, waiting for transfers between devices, local(): lax.psum(jnp.einsum('mik,mjk->mij', iterate, iterate, precision=lax.Preci...  116 us
    dot_general x4, matrix products, local(): jnp.einsum('mij,mjk->mik', mixed, iterate, precision=lax.Precision.HIGHEST)  55 us
    dot_general x4, matrix products, local(): jnp.einsum('mik,mjk->mij', iterate, iterate, precision=lax.Precision.HIGH...  38.5 us
    unnamed x8, local copies, waits for them, and re-layouts  13.6 us
  transfers between devices with their start and end apart: 4, of which 4 were waited for; matrix products, arithmetic and copies ran while one was open for 0% of the time, Pallas kernels for 0%

commit v1 on v0

v1 whole, which is shorter than its diff:
```python
import functools

import jax
import jax.numpy as jnp
from jax import lax
from jax.experimental import pallas as pl
from jax.experimental.pallas import tpu as pltpu
from jax.sharding import PartitionSpec as P

ITERS = 4

hold_rate = 0.9
learn_rate = 0.8

HIGHEST = lax.Precision.HIGHEST
MESH = pl.DeviceIdType.MESH
VMEM_LIMIT = 62 * 2**20


def polynomial(gram, total, mul, eye):
    scale = lax.rsqrt(total + 1e-06)
    a = gram * scale * scale
    factor = None
    for step in range(ITERS):
        p = 3.4445 * eye - 4.775 * a + 2.0315 * mul(a, a)
        factor = p if factor is None else mul(p, factor)
        if step < ITERS - 1:
            a = mul(mul(p, a), p)
    return factor * scale


def plain(gradients, momentum, weights):
    new_momentum = hold_rate * momentum + gradients
    direction = hold_rate * new_momentum + gradients
    moved = lax.all_to_all(direction, "shard", split_axis=0, concat_axis=1, tiled=True)
    gram = lax.psum(jnp.einsum("mik,mjk->mij", moved, moved, precision=HIGHEST), "model")
    eye = jnp.eye(gram.shape[-1], dtype=jnp.float32)
    total = jnp.sum(gram * eye, axis=(1, 2), keepdims=True)

    def mul(a, b):
        return jnp.einsum("mij,mjk->mik", a, b, precision=HIGHEST)

    iterate = mul(polynomial(gram, total, mul, eye), moved)
    back = lax.all_to_all(iterate, "shard", split_axis=1, concat_axis=0, tiled=True)
    return weights - learn_rate * back, new_momentum


def kernel(
    n, models, g_hbm, m_hbm, w_hbm, nw_hbm, nm_hbm,
    gbuf, mbuf, wbuf, rows_in, rows_out, back, grams,
    g_sem, m_sem, w_sem, nm_sem, nw_sem, send1, recv1, send2, recv2, gsend, grecv,
):
    me = lax.axis_index("shard")
    mine = lax.axis_index("model")
    per, _, r, cols = gbuf.shape
    side = n * r
    tile = min(512, cols)
    half = n // 2

    def peer(k):
        return lax.rem(me // half + 1 + k // half, 2) * half + lax.rem(me + k, half)

    partners = [k for k in range(n) if k != half]

    def load(j):
        return (
            pltpu.make_async_copy(g_hbm.at[:, j], gbuf.at[j], g_sem.at[j]),
            pltpu.make_async_copy(m_hbm.at[:, j], mbuf.at[j], m_sem.at[j]),
        )

    def load_w(j):
        return pltpu.make_async_copy(w_hbm.at[:, j], wbuf.at[j], w_sem.at[j])

    def put_nm(j):
        return pltpu.make_async_copy(mbuf.at[j], nm_hbm.at[:, j], nm_sem.at[j])

    def put_nw(j):
        return pltpu.make_async_copy(wbuf.at[j], nw_hbm.at[:, j], nw_sem.at[j])

    def scatter(src, dst, send, recv, j):
        for k in partners:
            to = peer(k)
            pltpu.make_async_remote_copy(
                src_ref=src.at[j, to],
                dst_ref=dst.at[j, me],
                send_sem=send.at[j],
                recv_sem=recv.at[j],
                device_id={"shard": to},
                device_id_type=MESH,
            ).start()

    def wait_all(buf, sem, j):
        whole = buf.at[j, pl.ds(0, n - 1)]
        pltpu.make_async_copy(whole, whole, sem.at[j]).wait()

    @pl.loop(0, per)
    def _(j):
        for copy in load(j):
            copy.start()

    barrier = pltpu.get_barrier_semaphore()
    for k in partners:
        pl.semaphore_signal(barrier, inc=1, device_id={"shard": peer(k)}, device_id_type=MESH)
    for k in range(1, models):
        pl.semaphore_signal(
            barrier, inc=1, device_id={"model": lax.rem(mine + k, models)}, device_id_type=MESH
        )
    pl.semaphore_wait(barrier, n - 1 + models - 1)

    @pl.loop(0, per)
    def _(j):
        for copy in load(j):
            copy.wait()

        @pl.loop(0, n)
        def _(d):
            g = gbuf[j, d]
            moment = hold_rate * mbuf[j, d] + g
            mbuf[j, d] = moment
            gbuf[j, d] = hold_rate * moment + g

        rows_in[j, me] = gbuf[j, me]
        scatter(gbuf, rows_in, send1, recv1, j)
        put_nm(j).start()
        load_w(j).start()

    row = lax.broadcasted_iota(jnp.int32, (side, side), 0)
    col = lax.broadcasted_iota(jnp.int32, (side, side), 1)
    eye = (row == col).astype(jnp.float32)

    def mul(a, b):
        return jnp.dot(a, b, precision=HIGHEST, preferred_element_type=jnp.float32)

    def columns(j, c):
        return rows_in[j, :, :, pl.ds(pl.multiple_of(c * tile, tile), tile)].reshape(side, tile)

    @pl.loop(0, per)
    def _(j):
        wait_all(rows_in, recv1, j)
        def add(c, total):
            x = columns(j, c)
            return total + lax.dot_general(
                x, x, (((1,), (1,)), ((), ())), precision=HIGHEST,
                preferred_element_type=jnp.float32,
            )

        grams[j, mine] = lax.fori_loop(
            0, cols // tile, add, jnp.zeros((side, side), jnp.float32)
        )
        for k in range(1, models):
            pltpu.make_async_remote_copy(
                src_ref=grams.at[j, mine],
                dst_ref=grams.at[j, mine],
                send_sem=gsend.at[j],
                recv_sem=grecv.at[j],
                device_id={"model": lax.rem(mine + k, models)},
                device_id_type=MESH,
            ).start()
        if models > 1:
            wait_all_grams = grams.at[j, pl.ds(0, models - 1)]
            pltpu.make_async_copy(wait_all_grams, wait_all_grams, grecv.at[j]).wait()
        gram = grams[j, 0]
        for k in range(1, models):
            gram = gram + grams[j, k]
        total = jnp.sum(jnp.sum(gram * eye, axis=1, keepdims=True), axis=0, keepdims=True)
        factor = polynomial(gram, total, mul, eye)

        @pl.loop(0, cols // tile)
        def _(c):
            rows_out[j, :, :, pl.ds(pl.multiple_of(c * tile, tile), tile)] = mul(
                factor, columns(j, c)
            ).reshape(n, r, tile)

        back[j, me] = rows_out[j, me]
        scatter(rows_out, back, send2, recv2, j)

    @pl.loop(0, per)
    def _(j):
        load_w(j).wait()
        wait_all(back, recv2, j)

        @pl.loop(0, n)
        def _(d):
            wbuf[j, d] = wbuf[j, d] - learn_rate * back[j, d]

        put_nw(j).start()

    @pl.loop(0, per)
    def _(j):
        put_nm(j).wait()
        put_nw(j).wait()
        wait_all(gbuf, send1, j)
        wait_all(rows_out, send2, j)
        if models > 1:
            sent = grams.at[j, pl.ds(0, models - 1)]
            pltpu.make_async_copy(sent, sent, gsend.at[j]).wait()


def local(n, models, gradients, momentum, weights):
    mats, r, cols = gradients.shape
    if r % 8 or cols % 128 or mats % n or n % 2 or gradients.nbytes * 6 > 50 * 2**20:
        return plain(gradients, momentum, weights)
    per = mats // n
    side = n * r
    shape = (n, per, r, cols)
    whole = pltpu.VMEM((per, n, r, cols), jnp.float32)
    flops = 6 * per * (4 * side * side * cols + 26 * side**3)
    any_spec = pl.BlockSpec(memory_space=pl.ANY)
    new_weights, new_momentum = pl.pallas_call(
        functools.partial(kernel, n, models),
        out_shape=(jax.ShapeDtypeStruct(shape, jnp.float32),) * 2,
        in_specs=[any_spec] * 3,
        out_specs=(any_spec,) * 2,
        scratch_shapes=[whole] * 6
        + [pltpu.VMEM((per, models, side, side), jnp.float32)]
        + [pltpu.SemaphoreType.DMA((per,))] * 11,
        compiler_params=pltpu.CompilerParams(
            collective_id=0, has_side_effects=True, vmem_limit_bytes=VMEM_LIMIT
        ),
        cost_estimate=pl.CostEstimate(
            flops=flops, bytes_accessed=5 * gradients.nbytes, transcendentals=0
        ),
    )(gradients.reshape(shape), momentum.reshape(shape), weights.reshape(shape))
    return new_weights.reshape(mats, r, cols), new_momentum.reshape(mats, r, cols)


def solution(mesh):
    spec = P(None, "shard", "model")
    return jax.shard_map(
        functools.partial(local, mesh.shape["shard"], mesh.shape["model"]),
        mesh=mesh,
        in_specs=(spec,) * 3,
        out_specs=(spec,) * 2,
        check_vma=False,
    )
```

time: 675 us -> 382 us (0.57); the launches traced: 666 us -> 382 us
  blocking collectives: 382 us -> 0 us
  Pallas kernels: 0 us -> 370 us
  waiting for transfers between devices: 116 us -> 0 us
  matrix products: 102 us -> 0 us
  other arithmetic: 23.8 us -> 0 us
  local copies, waits for them, and re-layouts: 28.1 us -> 11.4 us
  between operations: 14.3 us -> 0.65 us
    all_to_all x2 -> x0, blocking collectives: 377 us -> none  [the longest x1 189 us: local(): lax.all_to_all(direction, 'shard', split_axis=0, concat_axis=1, tiled=True)]
    pallas_call x0 -> x1, Pallas kernels: none -> 370 us  [local(): pl.pallas_call(functools.partial(kernel, n, models), out_shape=(jax.Shape...]
    psum x4 -> x0, waiting for transfers between devices: 116 us -> none  [local(): lax.psum(jnp.einsum('mik,mjk->mij', iterate, iterate, precision=lax.Preci...]
    dot_general x12 -> x0, matrix products: 102 us -> none  [the longest x4 55 us: local(): jnp.einsum('mij,mjk->mik', mixed, iterate, precision=lax.Precision.HIGHEST)]
    sub x1 -> x0, other arithmetic: 11.9 us -> none  [local(): new_weights = weights - learn_rate * back]
    mul x1 -> x0, local copies, waits for them, and re-layouts: 9.71 us -> none  [local(): new_weights = weights - learn_rate * back]
    add x1 -> x0, other arithmetic: 9.29 us -> none  [local(): direction = hold_rate * new_momentum + gradients]
    unnamed x8 -> x4, local copies, waits for them, and re-layouts: 13.6 us -> 11.4 us
  transfers between devices with their start and end apart: 4 -> 0, of which waited for: 4 -> 0; matrix products, arithmetic and copies ran while one was open for 0% -> 0% of each run, Pallas kernels for 0% -> 0%
where the time goes in v1:
time: 382 us
  Pallas kernels  370 us (97%)
  local copies, waits for them, and re-layouts  11.4 us (3%)
    pallas_call x1, Pallas kernels, local(): pl.pallas_call(functools.partial(kernel, n, models), out_shape=(jax.Shape...  370 us
    unnamed x4, local copies, waits for them, and re-layouts  11.4 us

profile of v1, /device:TPU:0, one launch (start us, length us, event | category | flops | bytes accessed | tf_op | source)
XLA Modules:
  0.0 382.1 jit_solution(8109004291918156037)
XLA Ops:
  0.6 370.0 %shard_map.50 = (f32[16,8,8,2048]{3,2,1,0:T(8,128)}, f32[16,8,8,2048]{3,2,1,0:T(8,128)}) custom-call(f32[16,8,8,2048]{3,2,1,0:T(8,128)} %bitcast.7, f32[16,8,8,2048]{3,2,1,0:T(8,128)} %bitcast.8, f32[16,8,8,2048]{3,2,1,0:T(8,128)} %bitcast.9), custom_call_target="tpu_custom_call" | custom-call | flops 9059696640 | bytes 41943040 | tf_op jit(solution)/shard_map/pallas_call | solution.py:209
  370.7 0.0 copy-start
  370.7 8.0 %copy.7 = f32[128,8,2048]{2,1,0:T(8,128)} copy(f32[128,8,2048]{2,1,0:T(8,128)} %bitcast.6) | data formatting | bytes 16777216
  378.7 0.0 copy-done
  378.7 3.4 copy.8
Async XLA Ops:
  370.7 8.1 %copy-start = (f32[16,8,8,2048]{3,2,1,0:T(8,128)S(1)}, f32[16,8,8,2048]{3,2,1,0:T(8,128)}, u32[]{:S(2)}) copy-start(f32[16,8,8,2048]{3,2,1,0:T(8,128)} %get-tuple-element.5) | copy-start | bytes 25165828

commit v2 on v1

--- a/solution.py
+++ b/solution.py
@@ -14,7 +14,6 @@
 
 HIGHEST = lax.Precision.HIGHEST
 MESH = pl.DeviceIdType.MESH
-VMEM_LIMIT = 62 * 2**20
 
 
 def polynomial(gram, total, mul, eye):
@@ -46,9 +45,9 @@
 
 
 def kernel(
-    n, models, g_hbm, m_hbm, w_hbm, nw_hbm, nm_hbm,
-    gbuf, mbuf, wbuf, rows_in, rows_out, back, grams,
-    g_sem, m_sem, w_sem, nm_sem, nw_sem, send1, recv1, send2, recv2, gsend, grecv,
+    n, models, g_hbm, m_hbm, w_hbm, wbuf, mbuf,
+    gbuf, rows_in, rows_out, back, grams,
+    g_sem, m_sem, w_sem, send1, recv1, send2, recv2, gsend, grecv,
 ):
     me = lax.axis_index("shard")
     mine = lax.axis_index("model")
@@ -60,22 +59,16 @@
     def peer(k):
         return lax.rem(me // half + 1 + k // half, 2) * half + lax.rem(me + k, half)
 
-    partners = [k for k in range(n) if k != half]
+    partners = [k for pair in zip(range(half), range(half, n)) for k in pair if k != half]
 
     def load(j):
         return (
             pltpu.make_async_copy(g_hbm.at[:, j], gbuf.at[j], g_sem.at[j]),
-            pltpu.make_async_copy(m_hbm.at[:, j], mbuf.at[j], m_sem.at[j]),
+            pltpu.make_async_copy(m_hbm.at[:, j], mbuf.at[:, j], m_sem.at[j]),
         )
 
     def load_w(j):
-        return pltpu.make_async_copy(w_hbm.at[:, j], wbuf.at[j], w_sem.at[j])
-
-    def put_nm(j):
-        return pltpu.make_async_copy(mbuf.at[j], nm_hbm.at[:, j], nm_sem.at[j])
-
-    def put_nw(j):
-        return pltpu.make_async_copy(wbuf.at[j], nw_hbm.at[:, j], nw_sem.at[j])
+        return pltpu.make_async_copy(w_hbm.at[:, j], wbuf.at[:, j], w_sem.at[j])
 
     def scatter(src, dst, send, recv, j):
         for k in partners:
@@ -93,10 +86,8 @@
         whole = buf.at[j, pl.ds(0, n - 1)]
         pltpu.make_async_copy(whole, whole, sem.at[j]).wait()
 
-    @pl.loop(0, per)
-    def _(j):
-        for copy in load(j):
-            copy.start()
+    for copy in load(0):
+        copy.start()
 
     barrier = pltpu.get_barrier_semaphore()
     for k in partners:
@@ -112,16 +103,20 @@
         for copy in load(j):
             copy.wait()
 
+        @pl.when(j + 1 < per)
+        def _():
+            for copy in load(j + 1):
+                copy.start()
+
         @pl.loop(0, n)
         def _(d):
             g = gbuf[j, d]
-            moment = hold_rate * mbuf[j, d] + g
-            mbuf[j, d] = moment
+            moment = hold_rate * mbuf[d, j] + g
+            mbuf[d, j] = moment
             gbuf[j, d] = hold_rate * moment + g
 
         rows_in[j, me] = gbuf[j, me]
         scatter(gbuf, rows_in, send1, recv1, j)
-        put_nm(j).start()
         load_w(j).start()
 
     row = lax.broadcasted_iota(jnp.int32, (side, side), 0)
@@ -181,19 +176,28 @@
 
         @pl.loop(0, n)
         def _(d):
-            wbuf[j, d] = wbuf[j, d] - learn_rate * back[j, d]
-
-        put_nw(j).start()
-
-    @pl.loop(0, per)
-    def _(j):
-        put_nm(j).wait()
-        put_nw(j).wait()
+            wbuf[d, j] = wbuf[d, j] - learn_rate * back[j, d]
+
+
+    @pl.loop(0, per)
+    def _(j):
         wait_all(gbuf, send1, j)
         wait_all(rows_out, send2, j)
         if models > 1:
             sent = grams.at[j, pl.ds(0, models - 1)]
             pltpu.make_async_copy(sent, sent, gsend.at[j]).wait()
+
+
+def write(a_ref, b_ref, a_out, b_out, sems):
+    copies = [
+        pltpu.make_async_copy(src.at[k], dst.at[k], sems.at[i, k])
+        for k in range(a_ref.shape[0])
+        for i, (src, dst) in enumerate(((a_ref, a_out), (b_ref, b_out)))
+    ]
+    for copy in copies:
+        copy.start()
+    for copy in copies:
+        copy.wait()
 
 
 def local(n, models, gradients, momentum, weights):
@@ -208,19 +212,27 @@
     any_spec = pl.BlockSpec(memory_space=pl.ANY)
     new_weights, new_momentum = pl.pallas_call(
         functools.partial(kernel, n, models),
-        out_shape=(jax.ShapeDtypeStruct(shape, jnp.float32),) * 2,
+        out_shape=(pltpu.VMEM(shape, jnp.float32),) * 2,
         in_specs=[any_spec] * 3,
-        out_specs=(any_spec,) * 2,
-        scratch_shapes=[whole] * 6
+        out_specs=(pl.BlockSpec(memory_space=pltpu.VMEM),) * 2,
+        scratch_shapes=[whole] * 4
         + [pltpu.VMEM((per, models, side, side), jnp.float32)]
-        + [pltpu.SemaphoreType.DMA((per,))] * 11,
+        + [pltpu.SemaphoreType.DMA((per,))] * 9,
         compiler_params=pltpu.CompilerParams(
-            collective_id=0, has_side_effects=True, vmem_limit_bytes=VMEM_LIMIT
+            collective_id=0, has_side_effects=True, vmem_limit_bytes=4 * gradients.nbytes + 6 * 2**20
         ),
         cost_estimate=pl.CostEstimate(
             flops=flops, bytes_accessed=5 * gradients.nbytes, transcendentals=0
         ),
     )(gradients.reshape(shape), momentum.reshape(shape), weights.reshape(shape))
+    new_weights, new_momentum = pl.pallas_call(
+        write,
+        out_shape=(jax.ShapeDtypeStruct(shape, jnp.float32),) * 2,
+        in_specs=[pl.BlockSpec(memory_space=pltpu.VMEM)] * 2,
+        out_specs=(any_spec,) * 2,
+        scratch_shapes=[pltpu.SemaphoreType.DMA((2, n))],
+        compiler_params=pltpu.CompilerParams(vmem_limit_bytes=3 * gradients.nbytes),
+    )(new_weights, new_momentum)
     return new_weights.reshape(mats, r, cols), new_momentum.reshape(mats, r, cols)
 
 

time: 382 us -> 375 us (0.982)
  local copies, waits for them, and re-layouts: 11.4 us -> 0 us
  Pallas kernels: 370 us -> 375 us
    unnamed x4 -> x0, local copies, waits for them, and re-layouts: 11.4 us -> none
    pallas_call x1 -> x2, Pallas kernels: 370 us -> 375 us  [the longest x1 369 us: local(): pl.pallas_call(functools.partial(kernel, n, models), out_shape=(pltpu.VME...]
where the time goes in v2:
time: 375 us
  Pallas kernels  375 us (100%)
    pallas_call x1, Pallas kernels, local(): pl.pallas_call(functools.partial(kernel, n, models), out_shape=(pltpu.VME...  369 us

profile of v2, /device:TPU:0, one launch (start us, length us, event | category | flops | bytes accessed | tf_op | source)
XLA Modules:
  0.0 375.3 jit_solution(6733991857526397952)
XLA Ops:
  0.6 368.6 %shard_map.50 = (f32[16,8,8,2048]{3,2,1,0:T(8,128)S(1)}, f32[16,8,8,2048]{3,2,1,0:T(8,128)S(1)}) custom-call(f32[16,8,8,2048]{3,2,1,0:T(8,128)} %bitcast.5, f32[16,8,8,2048]{3,2,1,0:T(8,128)} %bitcast.6, f32[16,8,8,2048]{3,2,1,0:T(8,128)} %bitcast.7), custom_call_target="tpu_custom_call" | custom-call | flops 9059696640 | bytes 41943040 | tf_op jit(solution)/shard_map/pallas_call | solution.py:213
  369.2 6.1 %shard_map.51 = (f32[16,8,8,2048]{3,2,1,0:T(8,128)}, f32[16,8,8,2048]{3,2,1,0:T(8,128)}) custom-call(f32[16,8,8,2048]{3,2,1,0:T(8,128)S(1)} %get-tuple-element.6.a_ref, f32[16,8,8,2048]{3,2,1,0:T(8,128)S(1)} %get-tuple-element.7.b_ref), custom_call_target="tpu_custom_call" | custom-call | tf_op jit(solution)/shard_map/pallas_call | solution.py:228
